TPU v7x, 32 devices: a whole 2x2x4 slice. The times are simulated.
32 devices in a mesh: groups: 2 (over y), ep: 4 (over z), tp: 2 (over x), dp: 2 (over core).
Axes of the slice: x: 2, y: 2, z: 4, core: 2. Of those that a mesh axis runs over, the one named last changes fastest.
Arguments:
- tokens: bfloat16 [512, 1536], P(('groups', 'ep', 'tp', 'dp')), parts along dimension 0, may hold values from -6 to 6
- expert_ids: int32 [512, 4], P(('groups', 'ep', 'tp', 'dp')), parts along dimension 0, may hold values from 0 to 7, all different within a row; in each aligned block of 16 rows (0 to 15, 16 to 31, ...) at most 16 rows name the same one
- gate_weights: float32 [512, 4], P(('groups', 'ep', 'tp', 'dp')), parts along dimension 0, may hold values from 0.1 to 1
- w_gate: bfloat16 [8, 1536, 1536], P(('ep', 'dp'), None, 'tp'), may hold values from -0.15625 to 0.15625
- w_up: bfloat16 [8, 1536, 1536], P(('ep', 'dp'), None, 'tp'), may hold values from -0.15625 to 0.15625
- w_down: bfloat16 [8, 1536, 1536], P(('ep', 'dp'), None, 'tp'), may hold values from -0.15625 to 0.15625
Outputs:
- mixed: bfloat16 [512, 1536], P(('groups', 'ep', 'tp', 'dp')), parts along dimension 0
- expert_loads: int32 [16], P('groups'), parts along dimension 0
There are 2 independent parts, one for each index of `groups`. A program takes and returns all parts, laid end to end along the dimension named above; an argument that names none is the same for every part. Nothing has to cross between parts.
Inputs may be any that keep to these rules, and one draw needn't show every extreme that they name: `expert_ids`: each row names 4 different experts. In each aligned block of 16 rows (the rows of one device) no expert is named by more than 16 rows, and in some blocks one expert is named by exactly 16 rows.
All inputs are finite; a program needn't handle non-finite values.
Results may differ from a plain program's by a relative error of at most 0.0057.
Values may be sent and summed in bfloat16 or wider, within the bound.
A program may use at most 64 MiB of HBM per device.

v0:
```python
import jax
import jax.numpy as jnp
from jax import lax
from jax.sharding import PartitionSpec as P


def expert_apply(token_rows, gate_part, up_part, down_part):
    gate_value = jnp.dot(token_rows, gate_part, preferred_element_type=jnp.float32)
    up_value = jnp.dot(token_rows, up_part, preferred_element_type=jnp.float32)
    hidden = (jax.nn.silu(gate_value) * up_value).astype(jnp.bfloat16)
    return lax.dot_general(
        hidden, down_part, (((1,), (1,)), ((), ())), preferred_element_type=jnp.float32
    )


def per_device(tokens, expert_ids, gate_weights, w_gate, w_up, w_down):
    tok_rows = tokens.shape[0]
    model_width = tokens.shape[1]
    top_count = expert_ids.shape[1]
    ep_count = lax.axis_size("ep")
    dp_count = lax.axis_size("dp")
    experts = ep_count * dp_count
    capacity = max(2, 2 * tok_rows * top_count // experts)
    pair_ids = expert_ids.reshape(-1)
    expert_range = jnp.arange(experts, dtype=jnp.int32)
    onehot = (pair_ids[:, None] == expert_range[None, :]).astype(jnp.int32)
    local_counts = jnp.sum(onehot, axis=0).astype(jnp.float32)
    expert_loads = lax.psum(local_counts, ("ep", "tp", "dp")).astype(jnp.int32)
    earlier = (jnp.cumsum(onehot, axis=0) - onehot) * onehot
    slot_ranks = jnp.sum(earlier, axis=1)
    targets = pair_ids * capacity + slot_ranks
    slot_range = jnp.arange(experts * capacity, dtype=jnp.int32)
    selector = jnp.any(
        targets.reshape(tok_rows, top_count)[None, :, :] == slot_range[:, None, None], axis=2
    )
    outgoing = jnp.dot(selector.astype(jnp.bfloat16), tokens, preferred_element_type=jnp.float32)
    outgoing = outgoing.astype(jnp.bfloat16).reshape(experts, capacity, model_width)
    arrived = lax.all_to_all(outgoing, ("ep", "dp"), split_axis=0, concat_axis=0, tiled=True)
    gate_local = w_gate[0]
    up_local = w_up[0]
    down_local = w_down[0]
    fragment = lax.all_gather(arrived, "tp", axis=0, tiled=True)
    flat_rows = fragment.reshape(-1, model_width)
    partial_value = expert_apply(flat_rows, gate_local, up_local, down_local)
    partial_terms = partial_value.reshape(fragment.shape[0], capacity, model_width)
    finished = lax.psum_scatter(partial_terms, "tp", scatter_dimension=0, tiled=True).astype(
        jnp.bfloat16
    )
    returned = lax.all_to_all(finished, ("ep", "dp"), split_axis=0, concat_axis=0, tiled=True)
    returned = returned.reshape(experts * capacity, model_width)
    picked = jnp.take(returned, targets, axis=0).reshape(tok_rows, top_count, model_width)
    mixed = jnp.sum(gate_weights[:, :, None] * picked.astype(jnp.float32), axis=1)
    return (mixed.astype(jnp.bfloat16), expert_loads)


def solution(mesh):
    return jax.shard_map(
        per_device,
        mesh=mesh,
        in_specs=(
            P(("groups", "ep", "tp", "dp"), None),
            P(("groups", "ep", "tp", "dp"), None),
            P(("groups", "ep", "tp", "dp"), None),
            P(("ep", "dp"), None, "tp"),
            P(("ep", "dp"), None, "tp"),
            P(("ep", "dp"), None, "tp"),
        ),
        out_specs=(P(("groups", "ep", "tp", "dp"), None), P("groups")),
        check_vma=False,
    )
```

profile of v0, /device:TPU:0, one launch (start us, length us, event | category | flops | bytes accessed | tf_op | source)
XLA Modules:
  0.0 120.0 jit_solution(3056895640101364888)
XLA Ops:
  7.2 0.0 copy-start
  7.2 0.0 reduce-scatter.2.cloned.1.call-start
  7.2 0.9 copy.18
  8.1 0.1 reshape.68
  8.2 0.1 fusion.12
  8.3 0.1 reduce_window_sum.11
  8.4 0.2 fusion.14
  8.6 0.1 reduce_sum.32
  8.7 0.1 copy.20
  8.8 0.1 fusion.13
  8.9 1.3 %convolution_convert_fusion = bf16[128,1536]{1,0:T(8,128)(2,1)S(1)} fusion(pred[128,16]{0,1:T(8,128)(4,1)S(1)} %fusion.13, bf16[16,1536]{1,0:T(8,128)(2,1)} %param.6), kind=kOutput, calls=%fused_computation.1 | convolution fusion | flops 6488064 | bytes 444416 | tf_op jit(solution)/shard_map/dot_general | solution.py:36
  10.1 18.7 %all_to_all.10 = bf16[8,16,1536]{2,1,0:T(8,128)(2,1)S(1)} all-to-all(bf16[8,16,1536]{2,1,0:T(8,128)(2,1)S(1)} %bitcast.30), channel_id=1, replica_groups=mesh['groups'=2,'ep'=4,'tp'=2,'dp'=2] {'ep','dp'}, dimensions={0} | all-to-all | bytes 786432 | tf_op jit(solution)/shard_map/all_to_all | solution.py:38
  28.8 11.4 %all_gather.3 = bf16[16,16,1536]{2,1,0:T(8,128)(2,1)S(1)} all-gather(bf16[8,16,1536]{2,1,0:T(8,128)(2,1)S(1)} %all_to_all.10), channel_id=1, replica_groups=mesh['groups'=2,'ep'=4,'tp'=2,'dp'=2] {'tp'}, dimensions={0}, use_global_device_ids=true | all-gather | bytes 1179648 | tf_op jit(solution)/shard_map/all_gather | solution.py:42
  40.2 0.0 copy-done.2
  40.2 0.8 fusion.4
  41.0 0.0 copy-done.3
  41.0 0.8 fusion.9
  41.8 0.0 copy-done
  41.9 2.0 %fusion = f32[16,16,1536]{2,1,0:T(8,128)} fusion(bf16[16,16,768]{2,1,0:T(8,128)(2,1)S(1)} %bitcast.33, bf16[1,1536,768]{2,1,0:T(8,128)(2,1)S(1)} %copy-done), kind=kOutput, calls=%fused_computation.2 | convolution fusion | flops 603979776 | bytes 4325376 | tf_op jit(solution)/shard_map/dot_general | solution.py:11
  43.8 0.0 reduce-scatter.2.cloned.1.call-update
  43.8 25.7 %reduce-scatter.2.cloned.1.call-done = f32[8,16,1536]{2,1,0:T(8,128)} async-done(((f32[16,16,1536]{2,1,0:T(8,128)}), f32[8,16,1536]{2,1,0:T(8,128)}) %reduce-scatter.2.cloned.1.call-update) | async-done | bytes 786448 | tf_op jit(solution)/shard_map/reduce_scatter | solution.py:46
  69.5 1.9 %convert_element_type.28 = bf16[8,16,1536]{2,1,0:T(8,128)(2,1)} convert(f32[8,16,1536]{2,1,0:T(8,128)} %reduce-scatter.2.cloned.1.call-done) | non-fusion elementwise | flops 196608 | bytes 1179648 | tf_op jit(solution)/shard_map/convert_element_type | solution.py:46
  71.4 4.6 %all-to-all-start.1 = ((bf16[8,16,1536]{2,1,0:T(8,128)(2,1)}), bf16[8,16,1536]{2,1,0:T(8,128)(2,1)S(1)}, u32[]{:S(2)}, u32[]{:S(2)}) async-start(bf16[8,16,1536]{2,1,0:T(8,128)(2,1)} %convert_element_type.28), calls=%async_computation.2 | async-start | bytes 786432 | tf_op jit(solution)/shard_map/all_to_all | solution.py:49
  76.0 34.5 %psum.7 = f32[8]{0:T(128)S(1)} all-reduce(f32[8]{0:T(128)S(1)} %convert_element_type.31), channel_id=1, replica_groups=mesh['groups'=2,'ep'=4,'tp'=2,'dp'=2] {'ep','tp','dp'}, use_global_device_ids=true, to_apply=%region_6.7 | all-reduce | flops 8 | bytes 64 | tf_op jit(solution)/shard_map/psum | solution.py:28
  110.5 0.1 mul.45
  110.6 0.0 copy-done.1
  110.6 0.1 copy.17
  110.7 0.5 convert_element_type.32
  111.3 0.0 all-to-all-done.1
  111.3 0.7 gather_fusion
  112.0 0.1 gather.7
  112.0 1.1 multiply_reduce_fusion
  (8 shorter events, 0.0 us)
Async XLA Ops:
  7.2 34.7 %copy-start = (bf16[1,1536,768]{2,1,0:T(8,128)(2,1)S(1)}, bf16[1,1536,768]{2,1,0:T(8,128)(2,1)}, u32[]{:S(2)}) copy-start(bf16[1,1536,768]{2,1,0:T(8,128)(2,1)} %param.11) | copy-start | bytes 7077892
  7.2 62.3 %reduce-scatter.2.cloned.1.call-start = ((), (), s32[]{:S(2)}) async-start(), calls=%async_computation.3 | async-start | bytes 2359296 | tf_op jit(solution)/shard_map/reduce_scatter | solution.py:46
  8.8 31.5 %copy-start.2 = (bf16[1,1536,768]{2,1,0:T(8,128)(2,1)S(1)}, bf16[1,1536,768]{2,1,0:T(8,128)(2,1)}, u32[]{:S(2)}) copy-start(bf16[1,1536,768]{2,1,0:T(8,128)(2,1)} %param.9) | copy-start | bytes 7077892
  28.8 12.2 %copy-start.3 = (bf16[1,1536,768]{2,1,0:T(8,128)(2,1)S(1)}, bf16[1,1536,768]{2,1,0:T(8,128)(2,1)}, u32[]{:S(2)}) copy-start(bf16[1,1536,768]{2,1,0:T(8,128)(2,1)} %param.10) | copy-start | bytes 7077892
  43.8 66.8 %copy-start.1 = (f32[16,4]{0,1:T(4,128)S(1)}, f32[16,4]{0,1:T(4,128)}, u32[]{:S(2)}) copy-start(f32[16,4]{0,1:T(4,128)} %param.8) | copy-start | bytes 772
  71.4 39.8 %all-to-all-start.1 = ((bf16[8,16,1536]{2,1,0:T(8,128)(2,1)}), bf16[8,16,1536]{2,1,0:T(8,128)(2,1)S(1)}, u32[]{:S(2)}, u32[]{:S(2)}) async-start(bf16[8,16,1536]{2,1,0:T(8,128)(2,1)} %convert_element_type.28), calls=%async_computation.2 | async-start | bytes 786432 | tf_op jit(solution)/shard_map/all_to_all | solution.py:49
Sparse Core Ops, SparseCore 0:
  44.0 25.4 reduce-scatter.1
where the time goes:
time: 120 us
  blocking collectives  64.6 us (54%)
  waiting for transfers between devices  25.7 us (21%)
  between operations  14.1 us (12%)
  matrix products  4.79 us (4%)
  starting transfers between devices  4.64 us (4%)
  other arithmetic  3.99 us (3%)
  local copies, waits for them, and re-layouts  2.12 us (2%)
    psum x1, blocking collectives, per_device(): expert_loads = lax.psum(local_counts, ('ep', 'tp', 'dp')).astype(jnp.int32)  34.5 us
    reduce_scatter x1, waiting for transfers between devices, per_device(): lax.psum_scatter(partial_terms, 'tp', scatter_dimension=0, tiled=True)  25.7 us
    all_to_all x1, blocking collectives, per_device(): lax.all_to_all(outgoing, ('ep', 'dp'), split_axis=0, concat_axis=0, tiled...  18.7 us
    all_gather x1, blocking collectives, per_device(): fragment = lax.all_gather(arrived, 'tp', axis=0, tiled=True)  11.4 us
    all_to_all x1, starting transfers between devices, per_device(): lax.all_to_all(finished, ('ep', 'dp'), split_axis=0, concat_axis=0, tiled...  4.6 us
  transfers between devices with their start and end apart: 2, of which 1 were waited for; matrix products, arithmetic and copies ran while one was open for 1% of the time, Pallas kernels for 0%

commit v1 on v0

--- a/solution.py
+++ b/solution.py
@@ -1,7 +1,272 @@
+import functools
+
 import jax
 import jax.numpy as jnp
 from jax import lax
+from jax.experimental import pallas as pl
+from jax.experimental.pallas import tpu as pltpu
 from jax.sharding import PartitionSpec as P
+
+MESH = pl.DeviceIdType.MESH
+LANES = 128
+STRIP = 512
+
+
+def nearest_order(ep_count):
+    rows = []
+    for own in range(ep_count):
+        others = [z for z in range(ep_count) if z != own]
+        rows.append(sorted(others, key=lambda z: (abs(z - own), z)))
+    return rows
+
+
+def pick(rows, own, position):
+    value = jnp.int32(rows[0][position])
+    for index in range(1, len(rows)):
+        value = jnp.where(own == index, jnp.int32(rows[index][position]), value)
+    return value
+
+
+def layer_kernel(
+    sizes,
+    tok_hbm, ids_hbm, gw_hbm, wg_hbm, wu_hbm, wd_hbm,
+    out_ref, loads_ref,
+    xall, ids_v, gw_v, wg, wu, wd, resf, resb, drecv, xsend, xrecv, zsend, zrecv,
+    local_sem, az_s, az_r, ax_s, ax_r, ad_s, ad_r, rd_s, rd_r, rx_s, rx_r, rz_s, rz_r,
+):
+    ep, tp, dp, rows, width, top, experts = sizes
+    z, x, c = lax.axis_index("ep"), lax.axis_index("tp"), lax.axis_index("dp")
+    order = nearest_order(ep)
+    z_peers = [pick(order, z, k) for k in range(ep - 1)]
+    x_peers = [lax.rem(x + k, tp) for k in range(1, tp)]
+    c_peers = [lax.rem(c + k, dp) for k in range(1, dp)]
+
+    tok_in = pltpu.make_async_copy(
+        tok_hbm, xall.at[x, c, z, :, pl.ds(0, width)], local_sem.at[0]
+    )
+    ids_in = pltpu.make_async_copy(ids_hbm, ids_v, local_sem.at[1])
+    gw_in = pltpu.make_async_copy(gw_hbm, gw_v, local_sem.at[2])
+    weights_in = [
+        pltpu.make_async_copy(src.at[0], dst, local_sem.at[3 + k])
+        for k, (src, dst) in enumerate(((wg_hbm, wg), (wu_hbm, wu), (wd_hbm, wd)))
+    ]
+    tok_in.start()
+    ids_in.start()
+    gw_in.start()
+    barrier = pltpu.get_barrier_semaphore()
+    targets = [{"ep": p} for p in z_peers] + [{"tp": p} for p in x_peers]
+    targets += [{"dp": p} for p in c_peers]
+    for target in targets:
+        pl.semaphore_signal(barrier, inc=1, device_id=target, device_id_type=MESH)
+    for copy in weights_in:
+        copy.start()
+
+    ids_in.wait()
+    gw_in.wait()
+    lane = lax.broadcasted_iota(jnp.int32, (rows, LANES), 1)
+    diagonal = lax.broadcasted_iota(jnp.int32, (rows, rows), 0)
+    diagonal = diagonal == lax.broadcasted_iota(jnp.int32, (rows, rows), 1)
+
+    def upright(row):
+        return jnp.sum(jnp.where(diagonal, row, 0.0), axis=1, keepdims=True)
+
+    meta = jnp.zeros((rows, LANES), jnp.float32)
+    for k in range(top):
+        gate = upright(gw_v[k : k + 1, :])
+        high = gate.astype(jnp.bfloat16).astype(jnp.float32)
+        middle = (gate - high).astype(jnp.bfloat16).astype(jnp.float32)
+        low = gate - high - middle
+        named = upright(ids_v[k : k + 1, :].astype(jnp.float32))
+        for position, part in enumerate((named, high, middle, low)):
+            meta = jnp.where(lane == position * top + k, part, meta)
+    xall[x, c, z, :, width:] = meta.astype(jnp.bfloat16)
+    tok_in.wait()
+    pl.semaphore_wait(barrier, len(targets))
+
+    def remote(src, dst, send, recv, target):
+        return pltpu.make_async_remote_copy(
+            src_ref=src, dst_ref=dst, send_sem=send, recv_sem=recv,
+            device_id=target, device_id_type=MESH,
+        )
+
+    def along_z(owner, target):
+        block = xall.at[x, c, owner]
+        return remote(block, block, az_s.at[target], az_r.at[owner], {"ep": target})
+
+    def along_x(column, owner, target):
+        block = xall.at[column, c, owner]
+        return remote(
+            block, block, ax_s.at[target, owner], ax_r.at[column, owner], {"tp": target}
+        )
+
+    def along_c(column, core, owner, target):
+        block = xall.at[column, core, owner]
+        return remote(
+            block, block, ad_s.at[target, column, owner], ad_r.at[core, column, owner],
+            {"dp": target},
+        )
+
+    sent = []
+
+    def go(copy):
+        copy.start()
+        sent.append(copy)
+
+    for p in z_peers:
+        go(along_z(z, p))
+    for p in x_peers:
+        go(along_x(x, z, p))
+    for p in c_peers:
+        go(along_c(x, c, z, p))
+    for p in z_peers:
+        along_z(p, p).wait_recv()
+        for q in x_peers:
+            go(along_x(x, p, q))
+        for q in c_peers:
+            go(along_c(x, c, p, q))
+
+    gathered = ep * dp * rows
+    mine = z * dp + c
+    loads = jnp.zeros((1, LANES), jnp.float32)
+    lanes_all = lax.broadcasted_iota(jnp.int32, (gathered, LANES), 1)
+
+    def apply(column, loads):
+        for q in c_peers:
+            for owner in [z] + z_peers:
+                along_c(column, q, owner, q).wait_recv()
+        flat = xall[column].reshape(gathered, width + LANES)
+        token_rows = flat[:, :width]
+        info = flat[:, width:].astype(jnp.float32)
+        scale = jnp.zeros((gathered, 1), jnp.float32)
+        for k in range(top):
+            named = info[:, k : k + 1].astype(jnp.int32)
+            loads = loads + jnp.sum(
+                (named == lanes_all).astype(jnp.float32), axis=0, keepdims=True
+            )
+            gate = info[:, top + k : top + k + 1] + info[:, 2 * top + k : 2 * top + k + 1]
+            gate = gate + info[:, 3 * top + k : 3 * top + k + 1]
+            scale = scale + jnp.where(named == mine, gate, 0.0)
+        gate_value = jnp.dot(token_rows, wg[...], preferred_element_type=jnp.float32)
+        up_value = jnp.dot(token_rows, wu[...], preferred_element_type=jnp.float32)
+        hidden = gate_value / (1.0 + jnp.exp(-gate_value)) * up_value
+        hidden = hidden.astype(jnp.bfloat16)
+        for first in range(0, width, STRIP):
+            cols = slice(first, first + STRIP)
+            value = lax.dot_general(
+                hidden, wd[cols, :], (((1,), (1,)), ((), ())),
+                preferred_element_type=jnp.float32,
+            )
+            value = (value * scale).reshape(dp, ep, rows, STRIP)
+            resf[column, :, :, :, cols] = value
+            resb[column, :, :, :, cols] = value.astype(jnp.bfloat16)
+        for q in c_peers:
+            go(over_c(column, c, q))
+        return loads
+
+    def over_c(column, core, target):
+        return remote(
+            resb.at[column, target], drecv.at[core, column],
+            rd_s.at[target, column], rd_r.at[core, column], {"dp": target},
+        )
+
+    def chip_sum(column, owner):
+        total = resf[column, c, owner]
+        for q in c_peers:
+            total = total + drecv[q, column, owner].astype(jnp.float32)
+        return total
+
+    def over_x(column, owner, target):
+        return remote(
+            xsend.at[target, owner], xrecv.at[column, owner],
+            rx_s.at[target, owner], rx_r.at[column, owner], {"tp": target},
+        )
+
+    def over_z(owner, target):
+        return remote(
+            zsend.at[target], zrecv.at[owner], rz_s.at[target], rz_r.at[owner],
+            {"ep": target},
+        )
+
+    for copy in weights_in:
+        copy.wait()
+    loads = apply(x, loads)
+    for p in x_peers:
+        for owner in [z] + z_peers:
+            along_x(p, owner, p).wait_recv()
+            for q in c_peers:
+                go(along_c(p, c, owner, q))
+    for p in x_peers:
+        loads = apply(p, loads)
+    loads_ref[...] = jnp.broadcast_to(loads, loads_ref.shape).astype(jnp.int32)
+
+    outward = z_peers[::-1] + [z]
+    for p in x_peers:
+        for q in c_peers:
+            over_c(p, q, q).wait_recv()
+        for owner in outward:
+            xsend[p, owner] = chip_sum(p, owner).astype(jnp.bfloat16)
+            go(over_x(x, owner, p))
+    for q in c_peers:
+        over_c(x, q, q).wait_recv()
+    total = None
+    for owner in outward:
+        total = chip_sum(x, owner)
+        for p in x_peers:
+            over_x(p, owner, p).wait_recv()
+            total = total + xrecv[p, owner].astype(jnp.float32)
+        if owner is not z:
+            zsend[owner] = total.astype(jnp.bfloat16)
+            go(over_z(z, owner))
+    for p in z_peers:
+        over_z(p, p).wait_recv()
+        total = total + zrecv[p].astype(jnp.float32)
+    out_ref[...] = total.astype(out_ref.dtype)
+    for copy in sent:
+        copy.wait_send()
+
+
+def fused_layer(tokens, expert_ids, gate_weights, w_gate, w_up, w_down):
+    rows, width = tokens.shape
+    top = expert_ids.shape[1]
+    ep, tp, dp = lax.axis_size("ep"), lax.axis_size("tp"), lax.axis_size("dp")
+    experts, hidden_part = ep * dp, w_gate.shape[2]
+    sizes = (ep, tp, dp, rows, width, top, experts)
+    bf16, f32, dma = jnp.bfloat16, jnp.float32, pltpu.SemaphoreType.DMA
+    mixed, loads = pl.pallas_call(
+        functools.partial(layer_kernel, sizes),
+        out_shape=(
+            jax.ShapeDtypeStruct((rows, width), bf16),
+            jax.ShapeDtypeStruct((8, LANES), jnp.int32),
+        ),
+        in_specs=[pl.BlockSpec(memory_space=pl.ANY)] * 6,
+        out_specs=[pl.BlockSpec(memory_space=pltpu.VMEM)] * 2,
+        scratch_shapes=[
+            pltpu.VMEM((tp, dp, ep, rows, width + LANES), bf16),
+            pltpu.VMEM((top, rows), jnp.int32),
+            pltpu.VMEM((top, rows), f32),
+            pltpu.VMEM((width, hidden_part), bf16),
+            pltpu.VMEM((width, hidden_part), bf16),
+            pltpu.VMEM((width, hidden_part), bf16),
+            pltpu.VMEM((tp, dp, ep, rows, width), f32),
+            pltpu.VMEM((tp, dp, ep, rows, width), bf16),
+            pltpu.VMEM((dp, tp, ep, rows, width), bf16),
+            pltpu.VMEM((tp, ep, rows, width), bf16),
+            pltpu.VMEM((tp, ep, rows, width), bf16),
+            pltpu.VMEM((ep, rows, width), bf16),
+            pltpu.VMEM((ep, rows, width), bf16),
+            dma((6,)),
+            dma((ep,)), dma((ep,)),
+            dma((tp, ep)), dma((tp, ep)),
+            dma((dp, tp, ep)), dma((dp, tp, ep)),
+            dma((dp, tp)), dma((dp, tp)),
+            dma((tp, ep)), dma((tp, ep)),
+            dma((ep,)), dma((ep,)),
+        ],
+        compiler_params=pltpu.CompilerParams(
+            collective_id=0, has_side_effects=True
+        ),
+    )(tokens, expert_ids.T, gate_weights.T, w_gate, w_up, w_down)
+    return mixed, loads[0, :experts]
 
 
 def expert_apply(token_rows, gate_part, up_part, down_part):
@@ -21,6 +286,8 @@
     dp_count = lax.axis_size("dp")
     experts = ep_count * dp_count
     capacity = max(2, 2 * tok_rows * top_count // experts)
+    if capacity >= tok_rows and experts <= LANES and 4 * top_count <= LANES:
+        return fused_layer(tokens, expert_ids, gate_weights, w_gate, w_up, w_down)
     pair_ids = expert_ids.reshape(-1)
     expert_range = jnp.arange(experts, dtype=jnp.int32)
     onehot = (pair_ids[:, None] == expert_range[None, :]).astype(jnp.int32)

time: 120 us -> 31.2 us (0.26)
  blocking collectives: 64.6 us -> 0 us
  Pallas kernels: 0 us -> 27.7 us
  waiting for transfers between devices: 25.7 us -> 0 us
  between operations: 14.1 us -> 0.64 us
  matrix products: 4.79 us -> 0 us
  starting transfers between devices: 4.64 us -> 0 us
  other arithmetic: 3.99 us -> 0 us
    psum x1 -> x0, blocking collectives: 34.5 us -> none  [per_device(): expert_loads = lax.psum(local_counts, ('ep', 'tp', 'dp')).astype(jnp.int32)]
    pallas_call x0 -> x1, Pallas kernels: none -> 27.7 us  [fused_layer(): pl.pallas_call(functools.partial(layer_kernel, sizes), out_shape=(jax.Sha...]
    reduce_scatter x1 -> x0, waiting for transfers between devices: 25.7 us -> none  [per_device(): lax.psum_scatter(partial_terms, 'tp', scatter_dimension=0, tiled=True)]
    all_to_all x1 -> x0, blocking collectives: 18.7 us -> none  [per_device(): lax.all_to_all(outgoing, ('ep', 'dp'), split_axis=0, concat_axis=0, tiled...]
    all_gather x1 -> x0, blocking collectives: 11.4 us -> none  [per_device(): fragment = lax.all_gather(arrived, 'tp', axis=0, tiled=True)]
    dot_general x4 -> x0, matrix products: 4.79 us -> none  [the longest x1 1.97 us: expert_apply(): lax.dot_general(hidden, down_part, (((1,), (1,)), ((), ())), preferred_el...]
    all_to_all x1 -> x0, starting transfers between devices: 4.6 us -> none  [per_device(): lax.all_to_all(finished, ('ep', 'dp'), split_axis=0, concat_axis=0, tiled...]
    convert_element_type x4 -> x0, other arithmetic: 2.5 us -> none  [the longest x1 1.91 us: per_device(): lax.psum_scatter(partial_terms, 'tp', scatter_dimension=0, tiled=True)]
  transfers between devices with their start and end apart: 2 -> 0, of which waited for: 1 -> 0; matrix products, arithmetic and copies ran while one was open for 1% -> 0% of each run, Pallas kernels for 0% -> 0%
where the time goes in v1:
time: 31.2 us; the launch traced here: 31 us
  Pallas kernels  27.7 us (89%)
  local copies, waits for them, and re-layouts  2.61 us (8%)
  between operations  0.64 us (2%)
    pallas_call x1, Pallas kernels, fused_layer(): pl.pallas_call(functools.partial(layer_kernel, sizes), out_shape=(jax.Sha...  27.7 us
    unnamed x1, local copies, waits for them, and re-layouts  1.42 us
    squeeze x1, local copies, waits for them, and re-layouts, fused_layer(): return (mixed, loads[0, :experts])  1.19 us

profile of v1, /device:TPU:0, one launch (start us, length us, event | category | flops | bytes accessed | tf_op | source)
XLA Modules:
  0.0 31.0 jit_solution(888569775642669639)
XLA Ops:
  0.6 27.7 %shard_map.77 = (bf16[16,1536]{1,0:T(8,128)(2,1)}, s32[8,128]{1,0:T(8,128)}) custom-call(bf16[16,1536]{1,0:T(8,128)(2,1)} %tok_hbm.1, s32[4,16]{1,0:T(4,128)} %bitcast.4, f32[4,16]{1,0:T(4,128)} %bitcast.5, bf16[1,1536,768]{2,1,0:T(8,128)(2,1)} %wg_hbm.1, bf16[1,1536,768]{2,1,0:T(8,128)(2,1)} %wu_hbm.1, bf16[1,1536,768]{2,1,0:T(8,128)(2,1)} %wd_hbm.1), custom_call_target="tpu_custom_call" | custom-call | tf_op jit(solution)/shard_map/pallas_call | solution.py:235
  28.4 1.2 %slice_bitcast_fusion = s32[8]{0:T(128)} fusion(s32[8,128]{1,0:T(8,128)} %get-tuple-element.5), kind=kLoop, calls=%fused_computation | loop fusion | bytes 64 | tf_op jit(solution)/shard_map/squeeze | solution.py:269
  29.6 1.4 %copy.9 = bf16[16,1536]{1,0:T(8,128)(2,1)} copy(bf16[16,1536]{1,0:T(8,128)(2,1)} %get-tuple-element.8) | data formatting | bytes 98304

commit v2 on v1

--- a/solution.py
+++ b/solution.py
@@ -32,7 +32,7 @@
     tok_hbm, ids_hbm, gw_hbm, wg_hbm, wu_hbm, wd_hbm,
     out_ref, loads_ref,
     xall, ids_v, gw_v, wg, wu, wd, resf, resb, drecv, xsend, xrecv, zsend, zrecv,
-    local_sem, az_s, az_r, ax_s, ax_r, ad_s, ad_r, rd_s, rd_r, rx_s, rx_r, rz_s, rz_r,
+    local_sem, az_s, az_r, ax_s, ax_r, ad_s, ad_r, rd_s, rd_r, rx_s, rx_r, rz_s, rz_r, entered,
 ):
     ep, tp, dp, rows, width, top, experts = sizes
     z, x, c = lax.axis_index("ep"), lax.axis_index("tp"), lax.axis_index("dp")
@@ -54,10 +54,20 @@
     ids_in.start()
     gw_in.start()
     barrier = pltpu.get_barrier_semaphore()
-    targets = [{"ep": p} for p in z_peers] + [{"tp": p} for p in x_peers]
-    targets += [{"dp": p} for p in c_peers]
-    for target in targets:
+    others = [{"tp": p} for p in x_peers] + [{"dp": p} for p in c_peers]
+    for target in others:
         pl.semaphore_signal(barrier, inc=1, device_id=target, device_id_type=MESH)
+    has_low, has_high = z > 0, z < ep - 1
+
+    @pl.when(has_low)
+    def _():
+        pl.semaphore_signal(barrier, inc=1, device_id={"ep": z - 1}, device_id_type=MESH)
+
+    @pl.when(has_high)
+    def _():
+        pl.semaphore_signal(barrier, inc=1, device_id={"ep": z + 1}, device_id_type=MESH)
+
+    greeted = len(others) + jnp.where(has_low, 1, 0) + jnp.where(has_high, 1, 0)
     for copy in weights_in:
         copy.start()
 
@@ -81,7 +91,7 @@
             meta = jnp.where(lane == position * top + k, part, meta)
     xall[x, c, z, :, width:] = meta.astype(jnp.bfloat16)
     tok_in.wait()
-    pl.semaphore_wait(barrier, len(targets))
+    pl.semaphore_wait(barrier, greeted)
 
     def remote(src, dst, send, recv, target):
         return pltpu.make_async_remote_copy(
@@ -112,12 +122,30 @@
         copy.start()
         sent.append(copy)
 
-    for p in z_peers:
-        go(along_z(z, p))
+    def pass_on(p):
+        @pl.when((p - z) * (p - z) > 1)
+        def _():
+            pl.semaphore_wait(entered.at[p], 1)
+
+        @pl.when((p < z) & has_high)
+        def _():
+            pl.semaphore_signal(
+                entered.at[p], inc=1, device_id={"ep": z + 1}, device_id_type=MESH
+            )
+
+        @pl.when((p > z) & has_low)
+        def _():
+            pl.semaphore_signal(
+                entered.at[p], inc=1, device_id={"ep": z - 1}, device_id_type=MESH
+            )
+
     for p in x_peers:
         go(along_x(x, z, p))
     for p in c_peers:
         go(along_c(x, c, z, p))
+    for p in z_peers:
+        pass_on(p)
+        go(along_z(z, p))
     for p in z_peers:
         along_z(p, p).wait_recv()
         for q in x_peers:
@@ -223,6 +251,11 @@
     out_ref[...] = total.astype(out_ref.dtype)
     for copy in sent:
         copy.wait_send()
+
+
+def finish_kernel(mixed_ref, loads_ref, out_ref, counts_ref):
+    out_ref[...] = mixed_ref[...]
+    counts_ref[...] = loads_ref[0, : counts_ref.shape[0]]
 
 
 def fused_layer(tokens, expert_ids, gate_weights, w_gate, w_up, w_down):
@@ -261,12 +294,22 @@
             dma((dp, tp)), dma((dp, tp)),
             dma((tp, ep)), dma((tp, ep)),
             dma((ep,)), dma((ep,)),
+            pltpu.SemaphoreType.REGULAR((ep,)),
         ],
         compiler_params=pltpu.CompilerParams(
             collective_id=0, has_side_effects=True
         ),
     )(tokens, expert_ids.T, gate_weights.T, w_gate, w_up, w_down)
-    return mixed, loads[0, :experts]
+    return pl.pallas_call(
+        finish_kernel,
+        out_shape=(
+            jax.ShapeDtypeStruct((rows, width), bf16),
+            jax.ShapeDtypeStruct((experts,), jnp.int32),
+        ),
+        in_specs=[pl.BlockSpec(memory_space=pltpu.VMEM)] * 2,
+        out_specs=[pl.BlockSpec(memory_space=pltpu.VMEM)] * 2,
+        compiler_params=pltpu.CompilerParams(vmem_limit_bytes=4 * 1024 * 1024),
+    )(mixed, loads)
 
 
 def expert_apply(token_rows, gate_part, up_part, down_part):

time: 31.2 us -> 30.4 us (0.974)
  local copies, waits for them, and re-layouts: 2.61 us -> 1.48 us
  Pallas kernels: 27.7 us -> 28.1 us
    squeeze x1 -> x0, local copies, waits for them, and re-layouts: 1.19 us -> none  [fused_layer(): return (mixed, loads[0, :experts])]
    pallas_call x0 -> x1, Pallas kernels: none -> 0.63 us  [fused_layer(): pl.pallas_call(finish_kernel, out_shape=(jax.ShapeDtypeStruct((rows, widt...]
    unnamed x1 -> x4, local copies, waits for them, and re-layouts: 1.42 us -> 1.48 us
where the time goes in v2:
time: 30.4 us; the launch traced here: 30.2 us
  Pallas kernels  28.1 us (92%)
  local copies, waits for them, and re-layouts  1.48 us (5%)
  between operations  0.65 us (2%)
    pallas_call x1, Pallas kernels, fused_layer(): pl.pallas_call(functools.partial(layer_kernel, sizes), out_shape=(jax.Sha...  27.5 us
    unnamed x4, local copies, waits for them, and re-layouts  1.48 us
    pallas_call x1, Pallas kernels, fused_layer(): pl.pallas_call(finish_kernel, out_shape=(jax.ShapeDtypeStruct((rows, widt...  0.63 us

profile of v2, /device:TPU:0, one launch (start us, length us, event | category | flops | bytes accessed | tf_op | source)
XLA Modules:
  0.0 30.2 jit_solution(14679007250509357248)
XLA Ops:
  0.6 27.5 %shard_map.77 = (bf16[16,1536]{1,0:T(8,128)(2,1)}, s32[8,128]{1,0:T(8,128)}) custom-call(bf16[16,1536]{1,0:T(8,128)(2,1)} %tok_hbm.1, s32[4,16]{1,0:T(4,128)} %bitcast.2, f32[4,16]{1,0:T(4,128)} %bitcast.3, bf16[1,1536,768]{2,1,0:T(8,128)(2,1)} %wg_hbm.1, bf16[1,1536,768]{2,1,0:T(8,128)(2,1)} %wu_hbm.1, bf16[1,1536,768]{2,1,0:T(8,128)(2,1)} %wd_hbm.1), custom_call_target="tpu_custom_call" | custom-call | tf_op jit(solution)/shard_map/pallas_call | solution.py:268
  28.1 0.0 copy-start
  28.1 0.8 %copy-done = bf16[16,1536]{1,0:T(8,128)(2,1)S(1)} copy-done((bf16[16,1536]{1,0:T(8,128)(2,1)S(1)}, bf16[16,1536]{1,0:T(8,128)(2,1)}, u32[]{:S(2)}) %copy-start) | copy-done | bytes 49176
  28.9 0.0 copy-start.1
  28.9 0.7 %copy-done.1 = s32[8,128]{1,0:T(8,128)S(1)} copy-done((s32[8,128]{1,0:T(8,128)S(1)}, s32[8,128]{1,0:T(8,128)}, u32[]{:S(2)}) %copy-start.1) | copy-done | bytes 4120
  29.6 0.6 %shard_map.78 = (bf16[16,1536]{1,0:T(8,128)(2,1)}, s32[8]{0:T(128)}) custom-call(bf16[16,1536]{1,0:T(8,128)(2,1)S(1)} %copy-done, s32[8,128]{1,0:T(8,128)S(1)} %copy-done.1), custom_call_target="tpu_custom_call" | custom-call | tf_op jit(solution)/shard_map/pallas_call | solution.py:303
Async XLA Ops:
  28.1 0.8 %copy-start = (bf16[16,1536]{1,0:T(8,128)(2,1)S(1)}, bf16[16,1536]{1,0:T(8,128)(2,1)}, u32[]{:S(2)}) copy-start(bf16[16,1536]{1,0:T(8,128)(2,1)} %get-tuple-element.4.mixed_ref) | copy-start | bytes 147460
  28.9 0.7 %copy-start.1 = (s32[8,128]{1,0:T(8,128)S(1)}, s32[8,128]{1,0:T(8,128)}, u32[]{:S(2)}) copy-start(s32[8,128]{1,0:T(8,128)} %get-tuple-element.5.loads_ref) | copy-start | bytes 12292
